TPU v7x, 512 devices: a 8x2x16 block of a 8x8x16 slice. The times are simulated.
512 devices in a mesh: groups: 2 (over y), rows: 16 (over z), sub: 8 (over x), pair: 2 (over core).
Axes of the slice: x: 8, y: 2, z: 16, core: 2. Of those that a mesh axis runs over, the one named last changes fastest.
The devices are a block of a 8x8x16 slice.
Arguments:
- embeddings: bfloat16 [131072, 1024], P(('groups', 'rows', 'sub', 'pair')), parts along dimension 0, may hold values from -80 to 80
- assignment: int32 [131072], P(('groups', 'rows', 'sub', 'pair')), parts along dimension 0, may hold values from 0 to 1023, as said below
- order: int32 [131072], P(('groups', 'rows', 'sub', 'pair')), parts along dimension 0, may hold values from 0 to 65535, each once
Outputs:
- max_similarity: float32 [131072], P(('groups', 'rows', 'sub', 'pair')), parts along dimension 0
- centre_distance: float32 [131072], P(('groups', 'rows', 'sub', 'pair')), parts along dimension 0
There are 2 independent parts, one for each index of `groups`. A program takes and returns all parts, laid end to end along the dimension named above; each array names one. Nothing has to cross between parts.
Inputs may be any that keep to these rules, and one draw needn't show every extreme that they name: `assignment`: cluster c belongs to owner c // 8, owners being numbered along rows then sub. In each aligned block of 256 rows (the rows of one device) at most 8 rows name clusters of one owner, and one owner receives exactly 8 from every block; no cluster is named more than 1 times in one block.
All inputs are finite; a program needn't handle non-finite values.
Results may differ from a plain program's by a relative error of at most 0.00063.
Values may be sent and summed in bfloat16 or wider, within the bound.
A program may use at most 64 MiB of HBM per device.

v0:
```python
import jax
import jax.numpy as jnp
from jax import lax
from jax.sharding import PartitionSpec as P

K = 1024


EPSILON = 1e-06


def in_blocks(x, dim, size):
    before, after = (x.shape[:dim], x.shape[dim + 1 :])
    return jnp.moveaxis(x.reshape(*before, size, -1, *after), dim, 0)


def joined_along(blocks, dim):
    blocks = jnp.moveaxis(blocks, 0, dim)
    dims = blocks.shape
    return blocks.reshape(*dims[:dim], dims[dim] * dims[dim + 1], *dims[dim + 2 :])


def exchange_both(x, axis, axes, splits, concats):
    sizes = [lax.axis_size(a) for a in axes]
    blocks = in_blocks(x, splits[0], sizes[0])
    blocks = jnp.moveaxis(in_blocks(blocks, splits[1] + 1, sizes[1]), 0, 1)
    inside = blocks.shape[2:]
    blocks = blocks.reshape(-1, *inside)
    blocks = lax.all_to_all(blocks, axis, split_axis=0, concat_axis=0, tiled=True)
    blocks = joined_along(blocks.reshape(*sizes, *inside), concats[0] + 1)
    return joined_along(blocks, concats[1])


def swapped(block, axis, stride):
    count = lax.axis_size(axis)
    route = []
    for low in range(count):
        high = low | 1 << stride
        if high != low and high < count:
            route += [(low, high), (high, low)]
    return lax.ppermute(block, axis, route)


def normalize(embeddings):
    values = embeddings.astype(jnp.float32)
    return (values * lax.rsqrt(jnp.sum(values * values, axis=1, keepdims=True) + EPSILON)).astype(
        jnp.bfloat16
    )


def block_terms(query_rows, query_cluster, query_order, key_rows, key_cluster, key_order):
    gram = lax.dot_general(
        query_rows, key_rows, (((1,), (1,)), ((), ())), preferred_element_type=jnp.float32
    )
    same = (query_cluster[:, None] == key_cluster[None, :]) & (key_cluster[None, :] >= 0)
    earlier = same & (key_order[None, :] < query_order[:, None])
    best_sim = jnp.max(jnp.where(earlier, gram, -1.0), axis=1)
    members = jnp.sum(same.astype(jnp.float32), axis=1)
    inner = jnp.sum(jnp.where(same, gram, 0.0), axis=1)
    return (gram, same, best_sim, members, inner)


def bucket_slots(assignment, per_bucket, buckets, capacity):
    bucket_of = assignment // per_bucket
    hits = (bucket_of[:, None] == jnp.arange(buckets, dtype=jnp.int32)[None, :]).astype(jnp.int32)
    within = jnp.sum(jnp.cumsum(hits, axis=0) * hits, axis=1) - 1
    return bucket_of * capacity + within


def per_device(embeddings, assignment, order):
    owners = lax.axis_size("rows") * lax.axis_size("sub")
    row_count = embeddings.shape[0]
    width = embeddings.shape[1]
    capacity = 4 * row_count // owners
    per_owner = K // owners
    total_slots = owners * capacity
    unit_rows = normalize(embeddings)
    slot_index = bucket_slots(assignment, per_owner, owners, capacity)
    send_rows = jnp.zeros((total_slots, width), jnp.bfloat16).at[slot_index].set(unit_rows)
    send_cluster = jnp.full((total_slots,), -1, jnp.int32).at[slot_index].set(assignment)
    send_order = jnp.zeros((total_slots,), jnp.int32).at[slot_index].set(order)
    across = lax.axis_size("rows")
    beside = lax.axis_size("sub")
    arrived = (
        exchange_both(
            send_rows.reshape(across, beside, capacity, width),
            ("rows", "sub"),
            ("rows", "sub"),
            (0, 1),
            (0, 1),
        ),
        exchange_both(
            send_cluster.reshape(across, beside, capacity),
            ("rows", "sub"),
            ("rows", "sub"),
            (0, 1),
            (0, 1),
        ),
        exchange_both(
            send_order.reshape(across, beside, capacity),
            ("rows", "sub"),
            ("rows", "sub"),
            (0, 1),
            (0, 1),
        ),
    )
    query_rows = arrived[0].reshape(total_slots, width)
    query_cluster = arrived[1].reshape(total_slots)
    query_order = arrived[2].reshape(total_slots)
    partner_rows, partner_cluster, partner_order = swapped(
        (query_rows, query_cluster, query_order), "pair", 0
    )
    own_gram, own_same, own_best, own_members, own_inner = block_terms(
        query_rows, query_cluster, query_order, query_rows, query_cluster, query_order
    )
    other_gram, other_same, other_best, other_members, other_inner = block_terms(
        query_rows, query_cluster, query_order, partner_rows, partner_cluster, partner_order
    )
    best_sim = jnp.maximum(own_best, other_best)
    members = jnp.maximum(own_members + other_members, 1.0)
    toward = (own_inner + other_inner) / members
    partner_toward = swapped(toward, "pair", 0)
    spread = (
        jnp.sum(jnp.where(own_same, toward[None, :], 0.0), axis=1)
        + jnp.sum(jnp.where(other_same, partner_toward[None, :], 0.0), axis=1)
    ) / members
    centre_dist = jnp.diagonal(own_gram) - 2.0 * toward + spread
    back_best, back_dist = (
        lax.all_to_all(best_sim, ("rows", "sub"), split_axis=0, concat_axis=0, tiled=True),
        lax.all_to_all(centre_dist, ("rows", "sub"), split_axis=0, concat_axis=0, tiled=True),
    )
    return (back_best[slot_index], back_dist[slot_index])


def solution(mesh):
    in_specs = (
        P(("groups", "rows", "sub", "pair"), None),
        P(("groups", "rows", "sub", "pair")),
        P(("groups", "rows", "sub", "pair")),
    )
    out_specs = (P(("groups", "rows", "sub", "pair")), P(("groups", "rows", "sub", "pair")))
    return jax.shard_map(
        per_device, mesh=mesh, in_specs=in_specs, out_specs=out_specs, check_vma=False
    )
```

profile of v0, /device:TPU:65, one launch (start us, length us, event | category | flops | bytes accessed | tf_op | source)
XLA Modules:
  0.0 300.2 jit_solution(9613228561731675015)
XLA Ops:
  0.6 0.7 fusion.19
  1.3 0.7 and_select_fusion
  2.0 0.1 copy.7
  2.1 0.2 fusion.6
  2.4 0.2 fusion.7
  2.6 0.7 compare_select_fusion
  3.3 1.2 fusion
  4.5 2.9 scatter_custom_fusion.2
  7.4 147.6 %all_to_all.33 = bf16[128,1,1,8,1024]{4,3,2,1,0:T(8,128)(2,1)} all-to-all(bf16[128,1,1,8,1024]{4,3,2,1,0:T(8,128)(2,1)S(1)} %bitcast.62), channel_id=1, replica_groups=mesh['groups'=2,'rows'=16,'sub'=8,'pair'=2] {'rows','sub'}, dimensions={0} | all-to-all | bytes 4194304 | tf_op jit(solution)/shard_map/all_to_all | solution.py:29
  155.0 6.6 %collective-permute-start.2 = (bf16[1024,1024]{1,0:T(8,128)(2,1)}, bf16[1024,1024]{1,0:T(8,128)(2,1)}, u32[]{:S(2)}, u32[]{:S(2)}) collective-permute-start(bf16[1024,1024]{1,0:T(8,128)(2,1)} %bitcast.20), channel_id=1, source_target_pairs={{0,1},{1,0},{2,3},{3,2},{4,5},{5,4},{6,7},{7,6},{8,9},{9,8},{10,11... | collective-permute-start | bytes 6291464 | tf_op jit(solution)/shard_map/ppermute | solution.py:41
  161.6 1.6 scatter_custom_fusion
  163.2 0.7 reshape_transpose_transpose_reshape_reshape_reshape.9
  163.9 12.7 %all-to-all-start = ((s32[128,1,1,8]{3,2,1,0:T(1,128)}), s32[128,1,1,8]{3,2,1,0:T(1,128)S(1)}, u32[]{:S(2)}, u32[]{:S(2)}) async-start(s32[128,1,1,8]{3,2,1,0:T(1,128)} %bitcast.4), calls=%async_computation | async-start | bytes 131072 | tf_op jit(solution)/shard_map/all_to_all | solution.py:29
  176.6 1.6 scatter_custom_fusion.1
  178.2 0.7 reshape_transpose_transpose_reshape_reshape_reshape.10
  178.9 10.8 %all-to-all-done = s32[128,1,1,8]{3,2,1,0:T(1,128)S(1)} async-done(((s32[128,1,1,8]{3,2,1,0:T(1,128)}), s32[128,1,1,8]{3,2,1,0:T(1,128)S(1)}, u32[]{:S(2)}, u32[]{:S(2)}) %all-to-all-start) | async-done | bytes 4128 | tf_op jit(solution)/shard_map/all_to_all | solution.py:29
  189.7 10.1 %all-to-all-start.1 = ((s32[128,1,1,8]{3,2,1,0:T(1,128)}), s32[128,1,1,8]{3,2,1,0:T(1,128)S(1)}, u32[]{:S(2)}, u32[]{:S(2)}) async-start(s32[128,1,1,8]{3,2,1,0:T(1,128)} %bitcast.9), calls=%async_computation.1 | async-start | bytes 131072 | tf_op jit(solution)/shard_map/all_to_all | solution.py:29
  199.8 0.1 eq.56
  199.9 3.5 %collective-permute-start = (s32[1024]{0:T(1024)S(1)}, s32[1024]{0:T(1024)S(1)}, u32[]{:S(2)}, u32[]{:S(2)}) collective-permute-start(s32[1024]{0:T(1024)S(1)} %eq.56), channel_id=1, source_target_pairs={{0,1},{1,0},{2,3},{3,2},{4,5},{5,4},{6,7},{7,6},{8,9},{9,8},{10,11... | collective-permute-start | bytes 12296 | tf_op jit(solution)/shard_map/ppermute | solution.py:41
  203.4 9.5 %all-to-all-done.1 = s32[128,1,1,8]{3,2,1,0:T(1,128)S(1)} async-done(((s32[128,1,1,8]{3,2,1,0:T(1,128)}), s32[128,1,1,8]{3,2,1,0:T(1,128)S(1)}, u32[]{:S(2)}, u32[]{:S(2)}) %all-to-all-start.1) | async-done | bytes 4128 | tf_op jit(solution)/shard_map/all_to_all | solution.py:29
  212.9 0.1 lt.17
  213.0 4.5 %collective-permute-start.1 = (s32[1024]{0:T(1024)S(1)}, s32[1024]{0:T(1024)S(1)}, u32[]{:S(2)}, u32[]{:S(2)}) collective-permute-start(s32[1024]{0:T(1024)S(1)} %lt.17), channel_id=1, source_target_pairs={{0,1},{1,0},{2,3},{3,2},{4,5},{5,4},{6,7},{7,6},{8,9},{9,8},{10,11... | collective-permute-start | bytes 12296 | tf_op jit(solution)/shard_map/ppermute | solution.py:41
  217.5 0.0 collective-permute-done
  217.5 4.6 %fusion.16 = f32[1024,1024]{0,1:T(8,128)S(1)} fusion(bf16[128,1,1,8,1024]{4,3,2,1,0:T(8,128)(2,1)} %all_to_all.33), kind=kOutput, calls=%fused_computation.51 | convolution fusion | flops 2147483648 | bytes 6291456 | tf_op jit(solution)/shard_map/dot_general | solution.py:52
  222.1 0.0 copy-start
  222.1 0.0 collective-permute-done.1
  222.1 0.0 collective-permute-done.2
  222.1 8.8 %select_reduce_fusion.2 = (f32[1024]{0:T(1024)S(1)}, f32[1024]{0:T(1024)S(1)}, f32[1024]{0:T(1024)S(1)}, f32[1024]{0:T(1024)S(1)}, f32[1024]{0:T(1024)S(1)}, /*index=5*/f32[1024]{0:T(1024)S(1)}) fusion(s32[1024]{0:T(1024)S(1)} %eq.56, s32[1024]{0:T(1024)S(1)} %collective-permute-done, pred[1024]{0:T(1024)(128)(4,1)S(1)} %broadcast_compare_fusion, ...), kind=kOutput, calls=%fused_computation.10 | convolution fusion | flops 2168449024 | bytes 8431616 | tf_op jit(solution)/shard_map/dot_general | solution.py:52
  230.9 0.0 copy-done
  231.0 2.0 collective-permute-start.3
  232.9 17.3 %gather_fusion.1 = f32[1024]{0:T(1024)S(1)} fusion(f32[1024,1024]{0,1:T(8,128)} %copy-done, s32[1024]{0:T(1024)S(1)} %bitcast.61), kind=kCustom, calls=%fused_computation.1 | custom fusion | bytes 16384 | tf_op jit(solution)/shard_map/jit(diagonal)/cond/branch_0_fun/gather | solution.py:127
  250.3 0.7 max.32
  251.0 10.1 %all-to-all-start.3 = ((f32[128,8,1]{1,2,0:T(1,128)}), f32[128,8,1]{1,2,0:T(1,128)S(1)}, u32[]{:S(2)}, u32[]{:S(2)}) async-start(f32[128,8,1]{1,2,0:T(1,128)} %bitcast.25), calls=%async_computation.3 | async-start | bytes 131072 | tf_op jit(solution)/shard_map/all_to_all | solution.py:129
  261.1 0.0 collective-permute-done.3
  261.1 2.2 select_reduce_fusion
  263.3 0.7 reshape.187
  264.0 10.0 %all-to-all-done.3 = f32[128,8,1]{1,2,0:T(1,128)S(1)} async-done(((f32[128,8,1]{1,2,0:T(1,128)}), f32[128,8,1]{1,2,0:T(1,128)S(1)}, u32[]{:S(2)}, u32[]{:S(2)}) %all-to-all-start.3) | async-done | bytes 4128 | tf_op jit(solution)/shard_map/all_to_all | solution.py:129
  274.1 10.2 %all-to-all-start.4 = ((f32[128,8,1]{1,2,0:T(1,128)}), f32[128,8,1]{1,2,0:T(1,128)S(1)}, u32[]{:S(2)}, u32[]{:S(2)}) async-start(f32[128,8,1]{1,2,0:T(1,128)} %bitcast.27), calls=%async_computation.4 | async-start | bytes 131072 | tf_op jit(solution)/shard_map/all_to_all | solution.py:130
  284.3 0.5 broadcast.119
  284.8 0.8 reduce.6
  285.6 0.1 all_to_all.25
  285.7 1.9 gather_fusion
  287.6 9.8 %all-to-all-done.4 = f32[128,8,1]{1,2,0:T(1,128)S(1)} async-done(((f32[128,8,1]{1,2,0:T(1,128)}), f32[128,8,1]{1,2,0:T(1,128)S(1)}, u32[]{:S(2)}, u32[]{:S(2)}) %all-to-all-start.4) | async-done | bytes 4128 | tf_op jit(solution)/shard_map/all_to_all | solution.py:130
  297.4 0.8 reduce.7
  298.2 0.1 all_to_all.27
  298.3 1.9 gather_fusion.2
  (14 shorter events, 0.1 us)
Async XLA Ops:
  155.0 67.1 %collective-permute-start.2 = (bf16[1024,1024]{1,0:T(8,128)(2,1)}, bf16[1024,1024]{1,0:T(8,128)(2,1)}, u32[]{:S(2)}, u32[]{:S(2)}) collective-permute-start(bf16[1024,1024]{1,0:T(8,128)(2,1)} %bitcast.20), channel_id=1, source_target_pairs={{0,1},{1,0},{2,3},{3,2},{4,5},{5,4},{6,7},{7,6},{8,9},{9,8},{10,11... | collective-permute-start | bytes 6291464 | tf_op jit(solution)/shard_map/ppermute | solution.py:41
  163.9 25.8 %all-to-all-start = ((s32[128,1,1,8]{3,2,1,0:T(1,128)}), s32[128,1,1,8]{3,2,1,0:T(1,128)S(1)}, u32[]{:S(2)}, u32[]{:S(2)}) async-start(s32[128,1,1,8]{3,2,1,0:T(1,128)} %bitcast.4), calls=%async_computation | async-start | bytes 131072 | tf_op jit(solution)/shard_map/all_to_all | solution.py:29
  189.7 23.2 %all-to-all-start.1 = ((s32[128,1,1,8]{3,2,1,0:T(1,128)}), s32[128,1,1,8]{3,2,1,0:T(1,128)S(1)}, u32[]{:S(2)}, u32[]{:S(2)}) async-start(s32[128,1,1,8]{3,2,1,0:T(1,128)} %bitcast.9), calls=%async_computation.1 | async-start | bytes 131072 | tf_op jit(solution)/shard_map/all_to_all | solution.py:29
  199.9 17.6 %collective-permute-start = (s32[1024]{0:T(1024)S(1)}, s32[1024]{0:T(1024)S(1)}, u32[]{:S(2)}, u32[]{:S(2)}) collective-permute-start(s32[1024]{0:T(1024)S(1)} %eq.56), channel_id=1, source_target_pairs={{0,1},{1,0},{2,3},{3,2},{4,5},{5,4},{6,7},{7,6},{8,9},{9,8},{10,11... | collective-permute-start | bytes 12296 | tf_op jit(solution)/shard_map/ppermute | solution.py:41
  213.0 9.1 %collective-permute-start.1 = (s32[1024]{0:T(1024)S(1)}, s32[1024]{0:T(1024)S(1)}, u32[]{:S(2)}, u32[]{:S(2)}) collective-permute-start(s32[1024]{0:T(1024)S(1)} %lt.17), channel_id=1, source_target_pairs={{0,1},{1,0},{2,3},{3,2},{4,5},{5,4},{6,7},{7,6},{8,9},{9,8},{10,11... | collective-permute-start | bytes 12296 | tf_op jit(solution)/shard_map/ppermute | solution.py:41
  222.1 8.9 %copy-start = (f32[1024,1024]{0,1:T(8,128)}, f32[1024,1024]{0,1:T(8,128)S(1)}, u32[]{:S(2)}) copy-start(f32[1024,1024]{0,1:T(8,128)S(1)} %fusion.16) | copy-start | bytes 12582916
  231.0 30.2 %collective-permute-start.3 = (f32[1024]{0:T(1024)S(1)}, f32[1024]{0:T(1024)S(1)}, u32[]{:S(2)}, u32[]{:S(2)}) collective-permute-start(f32[1024]{0:T(1024)S(1)} %add_divide_fusion), channel_id=1, source_target_pairs={{0,1},{1,0},{2,3},{3,2},{4,5},{5,4},{6,7},{7,6},{8,9},{9,8},{10,11... | collective-permute-start | bytes 12296 | tf_op jit(solution)/shard_map/ppermute | solution.py:41
  251.0 23.1 %all-to-all-start.3 = ((f32[128,8,1]{1,2,0:T(1,128)}), f32[128,8,1]{1,2,0:T(1,128)S(1)}, u32[]{:S(2)}, u32[]{:S(2)}) async-start(f32[128,8,1]{1,2,0:T(1,128)} %bitcast.25), calls=%async_computation.3 | async-start | bytes 131072 | tf_op jit(solution)/shard_map/all_to_all | solution.py:129
  274.1 23.3 %all-to-all-start.4 = ((f32[128,8,1]{1,2,0:T(1,128)}), f32[128,8,1]{1,2,0:T(1,128)S(1)}, u32[]{:S(2)}, u32[]{:S(2)}) async-start(f32[128,8,1]{1,2,0:T(1,128)} %bitcast.27), calls=%async_computation.4 | async-start | bytes 131072 | tf_op jit(solution)/shard_map/all_to_all | solution.py:130
where the time goes:
time: 303 us; the launch traced here: 300 us
  blocking collectives  148 us (49%)
  starting transfers between devices  59.6 us (20%)
  waiting for transfers between devices  40.1 us (13%)
  local copies, waits for them, and re-layouts  28.1 us (9%)
  matrix products  13.4 us (4%)
  other arithmetic  10.5 us (3%)
    all_to_all x1, blocking collectives, exchange_both(): lax.all_to_all(blocks, axis, split_axis=0, concat_axis=0, tiled=True)  148 us
    all_to_all x2, starting transfers between devices, exchange_both(): lax.all_to_all(blocks, axis, split_axis=0, concat_axis=0, tiled=True)  22.8 us
    all_to_all x2, waiting for transfers between devices, exchange_both(): lax.all_to_all(blocks, axis, split_axis=0, concat_axis=0, tiled=True)  20.3 us
    gather x1, local copies, waits for them, and re-layouts, per_device(): centre_dist = jnp.diagonal(own_gram) - 2.0 * toward + spread  17.3 us
    ppermute x4, starting transfers between devices, swapped(): return lax.ppermute(block, axis, route)  16.5 us
    dot_general x2, matrix products, block_terms(): lax.dot_general(query_rows, key_rows, (((1,), (1,)), ((), ())), preferred...  13.4 us
    all_to_all x1, starting transfers between devices, per_device(): lax.all_to_all(centre_dist, ('rows', 'sub'), split_axis=0, concat_axis=0,...  10.2 us
    all_to_all x1, starting transfers between devices, per_device(): lax.all_to_all(best_sim, ('rows', 'sub'), split_axis=0, concat_axis=0, ti...  10.1 us
  transfers between devices with their start and end apart: 8, of which 4 were waited for; matrix products, arithmetic and copies ran while one was open for 11% of the time, Pallas kernels for 0%

commit v1 on v0

v1 whole, which is shorter than its diff:
```python
import functools

import jax
import jax.numpy as jnp
from jax import lax
from jax.experimental import pallas as pl
from jax.experimental.pallas import tpu as pltpu
from jax.sharding import PartitionSpec as P

EPSILON = 1e-06
LANES = 128
CLUSTERS = 1024
SLOTS = 2
FIRST_OWNER_ROW = 3
MESH = pl.DeviceIdType.MESH
F32 = jnp.float32
BF16 = jnp.bfloat16


def iota(shape, dim):
    return lax.broadcasted_iota(jnp.int32, shape, dim)


def drain(ref, sem):
    pltpu.make_async_copy(ref, ref, sem).wait()


def kernel(
    sizes,
    emb_ref,
    cluster_ref,
    order_ref,
    base_ref,
    best_ref,
    dist_ref,
    used_ref,
    rank_ref,
    flags_out,
    flags_in,
    table_in,
    table_out,
    used_in,
    used_out,
    send_rows,
    send_order,
    got_rows,
    got_order,
    send_back,
    got_back,
    ready,
    flag_send,
    flag_recv,
    table_send,
    table_recv,
    used_send,
    used_recv,
    rows_send,
    rows_recv,
    order_send,
    order_recv,
    back_send,
    back_recv,
):
    nz, nx, nc, owner_rows, first_owner = sizes
    side = nx * nc
    blocks = nz * side
    owners = owner_rows * side
    count, width = emb_ref.shape
    pieces = width // LANES
    z = lax.axis_index("rows")
    x = lax.axis_index("sub")
    c = lax.axis_index("pair")
    xc = x * nc + c
    me = z * side + xc
    my_place = (z - first_owner) * side + xc
    is_owner = (z >= first_owner) & (z < first_owner + owner_rows)

    def device(tz, txc):
        return {"rows": tz, "sub": txc // nc, "pair": lax.rem(txc, nc)}

    def beside(k):
        return lax.rem(xc + k, side)

    def signal(sem, tz, txc):
        pl.semaphore_signal(sem, inc=1, device_id=device(tz, txc), device_id_type=MESH)

    def remote(src, dst, send, recv, tz, txc):
        return pltpu.make_async_remote_copy(
            src_ref=src,
            dst_ref=dst,
            send_sem=send,
            recv_sem=recv,
            device_id=device(tz, txc),
            device_id_type=MESH,
        )

    barrier = pltpu.get_barrier_semaphore()

    @pl.loop(1, side)
    def _(k):
        signal(barrier, z, beside(k))

    signal(barrier, lax.rem(z + 1, nz), xc)
    signal(barrier, lax.rem(z + nz - 1, nz), xc)

    cluster = cluster_ref[...]
    high = cluster // LANES
    low = cluster - high * LANES
    groups = CLUSTERS // LANES
    is_high = iota((groups, count), 0) == high
    is_low = (iota((LANES, count), 0) == low).astype(F32).astype(BF16)
    flags_out[...] = lax.dot_general(
        is_high.astype(F32).astype(BF16),
        is_low,
        (((1,), (1,)), ((), ())),
        preferred_element_type=F32,
    )

    pl.semaphore_wait(barrier, side - 1 + 2)

    @pl.loop(1, side)
    def _(k):
        remote(flags_out, flags_in.at[xc], flag_send, flag_recv, z, beside(k)).start()

    flags_in[xc] = flags_out[...]

    values = emb_ref[...].astype(F32)
    unit = (
        values * lax.rsqrt(jnp.sum(values * values, axis=1, keepdims=True) + EPSILON)
    ).astype(BF16)

    drain(flags_in.at[pl.ds(0, side - 1)], flag_recv)
    named = jnp.max(flags_in[...], axis=0)

    @pl.when(z == 0)
    def _():
        table_in[...] = jnp.zeros_like(table_in)

    upper = (iota((LANES, LANES), 0) < iota((LANES, LANES), 1)).astype(F32).astype(BF16)

    @pl.when(z > 0)
    def _():
        drain(table_in, table_recv)

    before = table_in[...]
    fresh = jnp.where((named > 0.0) & (before == 0.0), 1.0, 0.0)
    taken = jnp.max(before, axis=(0, 1), keepdims=True)
    inside = jnp.dot(fresh.astype(BF16), upper, preferred_element_type=F32)
    totals = jnp.sum(fresh, axis=1, keepdims=True)
    above = jnp.sum(
        jnp.where(
            iota((groups, groups), 0) > iota((groups, groups), 1),
            jnp.transpose(jnp.broadcast_to(totals, (groups, LANES)))[0:1, 0:groups],
            0.0,
        ),
        axis=1,
        keepdims=True,
    )
    table = jnp.where(fresh > 0.0, taken + above + inside + 1.0, before)
    table_out[...] = table

    @pl.when(z < nz - 1)
    def _():
        remote(table_out, table_in, table_send, table_recv, z + 1, xc).start()

    @pl.when(is_owner)
    def _():
        @pl.loop(0, z)
        def _(tz):
            signal(ready.at[z], tz, xc)

    used = jnp.broadcast_to(jnp.max(table, axis=(0, 1), keepdims=True), used_out.shape)
    used_out[...] = used

    @pl.when(z == nz - 1)
    def _():
        used_in[...] = used

        @pl.loop(0, nz - 1)
        def _(tz):
            remote(used_out, used_in, used_send, used_recv, tz, xc).start()

    tens = jnp.floor(table * (1.0 / 32.0))
    both = jnp.concatenate([tens, table - tens * 32.0], axis=0).astype(BF16)
    found = jnp.dot(both, is_low, preferred_element_type=F32)
    found = found[0:groups] * 32.0 + found[groups:]
    rank = jnp.sum(jnp.where(is_high, found, 0.0), axis=0, keepdims=True) - 1.0
    rank_ref[...] = rank
    slot = rank - base_ref[...]
    place = iota((owners, count), 0).astype(F32) * float(SLOTS)
    wanted = [place + float(s) == slot for s in range(SLOTS)]
    tiles = [
        jnp.dot(w.astype(F32).astype(BF16), unit, preferred_element_type=F32)
        for w in wanted
    ]
    send_rows[...] = (
        jnp.concatenate(tiles, axis=1)
        .reshape(owners, SLOTS * pieces, LANES)
        .astype(BF16)
    )
    position = order_ref[...].astype(F32) + 1.0
    orders = [
        jnp.sum(jnp.where(w, position, 0.0), axis=1, keepdims=True) for w in wanted
    ]
    lane = iota((owners, LANES), 1)
    send_order[...] = jnp.where(lane < LANES // 2, orders[0], orders[1]).reshape(
        owners, 1, LANES
    )

    def deliver(t, tz, txc):
        place = t * side + txc
        remote(
            send_order.at[place], got_order.at[me], order_send, order_recv, tz, txc
        ).start()
        remote(
            send_rows.at[place], got_rows.at[me], rows_send, rows_recv, tz, txc
        ).start()

    @pl.loop(0, owner_rows)
    def _(t):
        tz = t + first_owner

        @pl.when(tz > z)
        def _():
            pl.semaphore_wait(ready.at[tz], 1)

        @pl.loop(1, side)
        def _(k):
            deliver(t, tz, beside(k))

        @pl.when(tz != z)
        def _():
            deliver(t, tz, xc)

    @pl.when(is_owner)
    def _():
        got_rows[me] = send_rows[my_place]
        got_order[me] = send_order[my_place]
        drain(got_order.at[pl.ds(0, blocks - 1)], order_recv)
        drain(got_rows.at[pl.ds(0, blocks - 1)], rows_recv)
        members = got_rows[...].reshape(blocks, SLOTS * width)
        stamps = got_order[...].reshape(blocks, LANES)
        flipped = jnp.transpose(stamps)
        answers = []
        for s in range(SLOTS):
            rows = members[:, s * width : (s + 1) * width]
            at = s * (LANES // SLOTS)
            mine = stamps[:, at : at + 1]
            theirs = flipped[at : at + 1, :]
            gram = lax.dot_general(
                rows, rows, (((1,), (1,)), ((), ())), preferred_element_type=F32
            )
            earlier = (theirs > 0.0) & (theirs < mine)
            answers.append(
                jnp.max(jnp.where(earlier, gram, -1.0), axis=1, keepdims=True)
            )
            total = jnp.sum(
                jnp.where(theirs > 0.0, 1.0, 0.0), axis=1, keepdims=True
            )
            summed = jnp.dot(
                jnp.ones((8, blocks), BF16), rows, preferred_element_type=F32
            )[0:1]
            centre = summed / jnp.maximum(total, 1.0)
            offset = rows.astype(F32) - centre
            answers.append(jnp.sum(offset * offset, axis=1, keepdims=True))
        part = iota((blocks, LANES), 1) // (LANES // len(answers))
        answer = answers[-1]
        for n in range(len(answers) - 1):
            answer = jnp.where(part == n, answers[n], answer)
        send_back[...] = answer.reshape(blocks, 1, LANES)

        @pl.loop(0, nz)
        def _(tz):
            @pl.loop(1, side)
            def _(k):
                remote(
                    send_back.at[tz * side + beside(k)],
                    got_back.at[my_place],
                    back_send,
                    back_recv,
                    tz,
                    beside(k),
                ).start()

            @pl.when(tz != z)
            def _():
                remote(
                    send_back.at[tz * side + xc],
                    got_back.at[my_place],
                    back_send,
                    back_recv,
                    tz,
                    xc,
                ).start()

        got_back[my_place] = send_back[me]
        drain(got_back.at[pl.ds(0, owners - 1)], back_recv)

    @pl.when(jnp.logical_not(is_owner))
    def _():
        drain(got_back, back_recv)

    back = got_back[...].reshape(owners, LANES)
    step = LANES // (2 * SLOTS)
    best = jnp.zeros((1, count), F32)
    dist = jnp.zeros((1, count), F32)
    for s in range(SLOTS):
        at = 2 * s * step
        best += jnp.sum(
            jnp.where(wanted[s], back[:, at : at + 1], 0.0), axis=0, keepdims=True
        )
        dist += jnp.sum(
            jnp.where(wanted[s], back[:, at + step : at + step + 1], 0.0),
            axis=0,
            keepdims=True,
        )
    best_ref[...] = best
    dist_ref[...] = dist

    @pl.when(z < nz - 1)
    def _():
        drain(used_in, used_recv)
        drain(table_out, table_send)

    @pl.when(z == nz - 1)
    def _():
        @pl.loop(0, nz - 1)
        def _(tz):
            drain(used_out, used_send)

    used_ref[...] = used_in[...]
    drain(flags_in.at[pl.ds(0, side - 1)], flag_send)

    @pl.when(is_owner)
    def _():
        drain(send_rows.at[pl.ds(0, owners - 1)], rows_send)
        drain(send_order.at[pl.ds(0, owners - 1)], order_send)
        drain(send_back.at[pl.ds(0, blocks - 1)], back_send)

    @pl.when(jnp.logical_not(is_owner))
    def _():
        drain(send_rows, rows_send)
        drain(send_order, order_send)


def one_round(sizes, embeddings, cluster, order, base):
    nz, nx, nc, owner_rows, _ = sizes
    side = nx * nc
    blocks = nz * side
    owners = owner_rows * side
    count, width = embeddings.shape
    tiles = SLOTS * width // LANES
    groups = CLUSTERS // LANES
    vmem = pl.BlockSpec(memory_space=pltpu.VMEM)
    row = jax.ShapeDtypeStruct((1, count), F32)
    dma = pltpu.SemaphoreType.DMA
    return pl.pallas_call(
        functools.partial(kernel, sizes),
        out_shape=(row, row, jax.ShapeDtypeStruct((1, LANES), F32), row),
        in_specs=[vmem] * 4,
        out_specs=(vmem,) * 4,
        scratch_shapes=[
            pltpu.VMEM((groups, LANES), F32),
            pltpu.VMEM((side, groups, LANES), F32),
            pltpu.VMEM((groups, LANES), F32),
            pltpu.VMEM((groups, LANES), F32),
            pltpu.VMEM((1, LANES), F32),
            pltpu.VMEM((1, LANES), F32),
            pltpu.VMEM((owners, tiles, LANES), BF16),
            pltpu.VMEM((owners, 1, LANES), F32),
            pltpu.VMEM((blocks, tiles, LANES), BF16),
            pltpu.VMEM((blocks, 1, LANES), F32),
            pltpu.VMEM((blocks, 1, LANES), F32),
            pltpu.VMEM((owners, 1, LANES), F32),
            pltpu.SemaphoreType.REGULAR((nz,)),
        ]
        + [dma] * 12,
        compiler_params=pltpu.CompilerParams(collective_id=0, has_side_effects=True),
    )(embeddings, cluster, order, base)


def per_device(embeddings, assignment, order):
    nz, nx, nc = (lax.axis_size(a) for a in ("rows", "sub", "pair"))
    count = embeddings.shape[0]
    capacity = count + count // 4
    owner_rows = capacity // (SLOTS * nx * nc)
    capacity = owner_rows * SLOTS * nx * nc
    sizes = (nz, nx, nc, owner_rows, FIRST_OWNER_ROW)
    run = functools.partial(
        one_round,
        sizes,
        embeddings,
        assignment.reshape(1, count),
        order.reshape(1, count),
    )
    best, dist, used, _ = run(jnp.zeros((1, count), F32))

    def unfinished(state):
        return state[2] < used[0, 0]

    def next_round(state):
        best, dist, base = state
        more_best, more_dist, _, rank = run(jnp.full((1, count), base))
        late = (rank >= base) & (rank < base + capacity)
        return (
            jnp.where(late, more_best, best),
            jnp.where(late, more_dist, dist),
            base + capacity,
        )

    best, dist, _ = lax.while_loop(
        unfinished, next_round, (best, dist, jnp.float32(capacity))
    )
    return best.reshape(count), dist.reshape(count)


def solution(mesh):
    in_specs = (
        P(("groups", "rows", "sub", "pair"), None),
        P(("groups", "rows", "sub", "pair")),
        P(("groups", "rows", "sub", "pair")),
    )
    out_specs = (P(("groups", "rows", "sub", "pair")), P(("groups", "rows", "sub", "pair")))
    return jax.shard_map(
        per_device, mesh=mesh, in_specs=in_specs, out_specs=out_specs, check_vma=False
    )
```

time: 303 us -> 150 us (0.50)
  blocking collectives: 148 us -> 0 us
  Pallas kernels: 0 us -> 146 us
  starting transfers between devices: 59.6 us -> 0 us
  waiting for transfers between devices: 40.1 us -> 0 us
  local copies, waits for them, and re-layouts: 28.1 us -> 2.97 us
  matrix products: 13.4 us -> 0 us
  other arithmetic: 10.5 us -> 0 us
    all_to_all x1 -> x0, blocking collectives: 148 us -> none  [exchange_both(): lax.all_to_all(blocks, axis, split_axis=0, concat_axis=0, tiled=True)]
    pallas_call x0 -> x1, Pallas kernels: none -> 146 us  [one_round(): pl.pallas_call(functools.partial(kernel, sizes), out_shape=(row, row, jax...]
    all_to_all x4 -> x0, starting transfers between devices: 43.1 us -> none  [the longest x2 22.8 us: exchange_both(): lax.all_to_all(blocks, axis, split_axis=0, concat_axis=0, tiled=True)]
    all_to_all x4 -> x0, waiting for transfers between devices: 40.1 us -> none  [the longest x2 20.3 us: exchange_both(): lax.all_to_all(blocks, axis, split_axis=0, concat_axis=0, tiled=True)]
    gather x3 -> x0, local copies, waits for them, and re-layouts: 21.2 us -> none  [the longest x1 17.3 us: per_device(): centre_dist = jnp.diagonal(own_gram) - 2.0 * toward + spread]
    ppermute x4 -> x0, starting transfers between devices: 16.5 us -> none  [swapped(): return lax.ppermute(block, axis, route)]
    dot_general x2 -> x0, matrix products: 13.4 us -> none  [block_terms(): lax.dot_general(query_rows, key_rows, (((1,), (1,)), ((), ())), preferred...]
    reduce_sum x3 -> x0, other arithmetic: 3.57 us -> none  [the longest x1 2.17 us: per_device(): jnp.sum(jnp.where(other_same, partner_toward[None, :], 0.0), axis=1)]
  transfers between devices with their start and end apart: 8 -> 0, of which waited for: 4 -> 0; matrix products, arithmetic and copies ran while one was open for 11% -> 0% of each run, Pallas kernels for 0% -> 0%
where the time goes in v1:
time: 150 us
  Pallas kernels  146 us (97%)
  local copies, waits for them, and re-layouts  2.97 us (2%)
    pallas_call x1, Pallas kernels, one_round(): pl.pallas_call(functools.partial(kernel, sizes), out_shape=(row, row, jax...  146 us

profile of v1, /device:TPU:65, one launch (start us, length us, event | category | flops | bytes accessed | tf_op | source)
XLA Modules:
  0.0 150.1 jit_solution(14927594570749526101)
XLA Ops:
  0.6 0.0 copy-start
  0.6 0.6 broadcast_in_dim.6.base_ref
  1.2 146.4 %shard_map.50 = (f32[1,256]{1,0:T(1,128)S(1)}, f32[1,256]{1,0:T(1,128)S(1)}, f32[1,128]{1,0:T(1,128)}, f32[1,256]{1,0:T(1,128)}) custom-call(bf16[256,1024]{1,0:T(8,128)(2,1)} %emb_ref.1, s32[1,256]{1,0:T(1,128)} %bitcast.8, s32[1,256]{1,0:T(1,128)} %bitcast.10, f32[1,256]{1,0:T(1,128)} %broadcast_in_dim.6.base_ref), custom_call_target="tpu_custom_call" | custom-call | tf_op jit(solution)/shard_map/pallas_call | solution.py:357
  147.6 0.0 copy-start.2
  147.6 0.0 copy-start.1
  147.6 0.0 copy-done
  147.6 0.6 copy-done.2
  148.3 0.0 copy-done.1
  148.3 0.6 while.12
  148.3 0.0 copy-start.6
  148.3 0.6 copy-done.6
  148.9 0.6 copy.16
  149.5 0.6 copy.17
Async XLA Ops:
  0.6 147.0 %copy-start = (bf16[256,1024]{1,0:T(8,128)(2,1)S(1)}, bf16[256,1024]{1,0:T(8,128)(2,1)}, u32[]{:S(2)}) copy-start(bf16[256,1024]{1,0:T(8,128)(2,1)} %emb_ref.1) | copy-start | bytes 1572868
  147.6 0.7 copy-start.2
  147.6 0.7 copy-start.1
  148.3 0.6 copy-start.6

commit v2 on v1

v2 whole, which is shorter than its diff:
```python
import functools

import jax
import jax.numpy as jnp
from jax import lax
from jax.experimental import pallas as pl
from jax.experimental.pallas import tpu as pltpu
from jax.sharding import PartitionSpec as P

EPSILON = 1e-06
LANES = 128
CLUSTERS = 1024
SLOTS = 2
MESH = pl.DeviceIdType.MESH
F32 = jnp.float32
BF16 = jnp.bfloat16


def iota(shape, dim):
    return lax.broadcasted_iota(jnp.int32, shape, dim)


def padded(rows):
    return -(-rows // 8) * 8


def drain(ref, sem):
    pltpu.make_async_copy(ref, ref, sem).wait()


def kernel(
    sizes,
    emb_ref,
    cluster_ref,
    order_ref,
    base_ref,
    best_ref,
    dist_ref,
    used_ref,
    rank_ref,
    flags_out,
    flags_in,
    named,
    used_in,
    used_out,
    send_rows,
    order_out,
    order_mid,
    send_order,
    got_rows,
    got_order,
    answers,
    gathered,
    send_back,
    got_back,
    ready,
    next_in,
    named_recv,
    flag_send,
    flag_recv,
    named_send,
    used_send,
    used_recv,
    rows_send,
    rows_recv,
    mid_send,
    mid_recv,
    order_send,
    order_recv,
    answer_send,
    answer_recv,
    back_send,
    back_recv,
):
    nz, nx, nc, owner_rows = sizes
    side = nx * nc
    blocks = nz * side
    owners = owner_rows * side
    share = LANES // side
    pad = padded(owner_rows)
    count, width = emb_ref.shape
    pieces = width // LANES
    z = lax.rem(lax.axis_index("rows") + nz - 1, nz)
    x = lax.axis_index("sub")
    c = lax.axis_index("pair")
    xc = x * nc + c
    me = xc * nz + z
    owner_row = (z * owner_rows + nz - 1) // nz
    is_owner = (owner_row * nz) // owner_rows == z
    my_place = owner_row * side + xc

    def device(tz, txc):
        return {
            "rows": lax.rem(tz + 1, nz),
            "sub": txc // nc,
            "pair": lax.rem(txc, nc),
        }

    def beside(k):
        return lax.rem(xc + k, side)

    def signal(sem, tz, txc):
        pl.semaphore_signal(sem, inc=1, device_id=device(tz, txc), device_id_type=MESH)

    def remote(src, dst, send, recv, tz, txc):
        return pltpu.make_async_remote_copy(
            src_ref=src,
            dst_ref=dst,
            send_sem=send,
            recv_sem=recv,
            device_id=device(tz, txc),
            device_id_type=MESH,
        )

    barrier = pltpu.get_barrier_semaphore()

    @pl.loop(1, side)
    def _(k):
        signal(barrier, z, beside(k))

    @pl.when(z < nz - 1)
    def _():
        signal(barrier, z + 1, xc)

    cluster = cluster_ref[...]
    high = cluster // LANES
    low = cluster - high * LANES
    groups = CLUSTERS // LANES
    is_high = iota((groups, count), 0) == high
    is_low = (iota((LANES, count), 0) == low).astype(F32).astype(BF16)
    flags_out[...] = lax.dot_general(
        is_high.astype(F32).astype(BF16),
        is_low,
        (((1,), (1,)), ((), ())),
        preferred_element_type=F32,
    )

    pl.semaphore_wait(barrier, side - 1 + (z + nz - 1) // nz)

    @pl.when(z > 0)
    def _():
        signal(next_in, z - 1, xc)

    @pl.loop(1, side)
    def _(k):
        remote(flags_out, flags_in.at[xc], flag_send, flag_recv, z, beside(k)).start()

    flags_in[xc] = flags_out[...]

    values = emb_ref[...].astype(F32)
    unit = (
        values * lax.rsqrt(jnp.sum(values * values, axis=1, keepdims=True) + EPSILON)
    ).astype(BF16)

    drain(flags_in.at[pl.ds(0, side - 1)], flag_recv)
    named[z] = jnp.max(flags_in[...], axis=0)

    def pass_on(tz):
        @pl.when(z < nz - 1)
        def _():
            remote(
                named.at[tz], named.at[tz], named_send, named_recv.at[tz], z + 1, xc
            ).start()

    @pl.when(z < nz - 1)
    def _():
        pl.semaphore_wait(next_in, 1)

    @pl.loop(0, z)
    def _(tz):
        drain(named.at[tz], named_recv.at[tz])
        pass_on(tz)

        @pl.when(is_owner)
        def _():
            signal(ready.at[z], tz, xc)

    pass_on(z)

    seen = jnp.zeros((groups, LANES), F32)
    fresh = []
    for tz in range(nz):
        here = jnp.where(z >= tz, named[tz], 0.0)
        fresh.append(jnp.where((here > 0.0) & (seen == 0.0), 1.0, 0.0))
        seen = jnp.maximum(seen, here)
    firsts = jnp.concatenate(fresh, axis=0).astype(BF16)
    levels = nz * groups
    upper = (iota((LANES, LANES), 0) < iota((LANES, LANES), 1)).astype(F32).astype(BF16)
    lower = (iota((levels, levels), 0) > iota((levels, levels), 1)).astype(F32)
    inside = jnp.dot(firsts, upper, preferred_element_type=F32)
    above = jnp.sum(
        jnp.dot(lower.astype(BF16), firsts, preferred_element_type=F32),
        axis=1,
        keepdims=True,
    )
    ranks = inside + above + 1.0
    table = jnp.zeros((groups, LANES), F32)
    for tz in range(nz):
        table += fresh[tz] * ranks[tz * groups : (tz + 1) * groups]

    used = jnp.broadcast_to(jnp.max(table, axis=(0, 1), keepdims=True), used_out.shape)
    used_out[...] = used

    @pl.when(z == nz - 1)
    def _():
        used_in[...] = used

        @pl.loop(0, nz - 1)
        def _(tz):
            remote(used_out, used_in, used_send, used_recv, tz, xc).start()

    tens = jnp.floor(table * (1.0 / 32.0))
    both = jnp.concatenate([tens, table - tens * 32.0], axis=0).astype(BF16)
    found = jnp.dot(both, is_low, preferred_element_type=F32)
    found = found[0:groups] * 32.0 + found[groups:]
    rank = jnp.sum(jnp.where(is_high, found, 0.0), axis=0, keepdims=True) - 1.0
    rank_ref[...] = rank
    slot = rank if base_ref is None else rank - base_ref[...]
    place = iota((owners, count), 0).astype(F32) * float(SLOTS)
    wanted = [place + float(s) == slot for s in range(SLOTS)]
    tiles = [
        jnp.dot(w.astype(F32).astype(BF16), unit, preferred_element_type=F32)
        for w in wanted
    ]
    send_rows[...] = (
        jnp.concatenate(tiles, axis=1)
        .reshape(owners, SLOTS * pieces, LANES)
        .astype(BF16)
    )
    position = order_ref[...].astype(F32) + 1.0
    line = iota((side * pad, count), 0)
    at_row = lax.rem(line, pad)
    place = jnp.where(at_row < owner_rows, at_row * side + line // pad, -CLUSTERS)
    place = place.astype(F32) * float(SLOTS)
    orders = [
        jnp.sum(
            jnp.where(place + float(s) == slot, position, 0.0), axis=1, keepdims=True
        )
        for s in range(SLOTS)
    ]
    even = lax.rem(iota((side * pad, LANES), 1), SLOTS) == 0
    order_out[...] = jnp.where(even, orders[0], orders[1])

    @pl.loop(1, side, unroll=3)
    def _(k):
        remote(
            order_out.at[pl.ds(pl.multiple_of(beside(k) * pad, pad), pad)],
            order_mid.at[xc],
            mid_send,
            mid_recv,
            z,
            beside(k),
        ).start()

    order_mid[xc] = order_out[pl.ds(pl.multiple_of(xc * pad, pad), pad), :]

    def deliver(t, tz, txc):
        place = t * side + txc
        remote(
            send_rows.at[place], got_rows.at[me], rows_send, rows_recv, tz, txc
        ).start()

    @pl.loop(0, owner_rows)
    def _(t):
        tz = (t * nz) // owner_rows

        @pl.when(tz > z)
        def _():
            pl.semaphore_wait(ready.at[tz], 1)

        @pl.loop(1, side, unroll=5)
        def _(k):
            deliver(t, tz, beside(k))

        @pl.when(tz != z)
        def _():
            deliver(t, tz, xc)

    drain(order_mid.at[pl.ds(0, side - 1)], mid_recv)
    origin = iota((pad, LANES), 1) // share
    packed = order_mid[side - 1]
    for n in range(side - 1):
        packed = jnp.where(origin == n, order_mid[n], packed)
    send_order[...] = packed.reshape(pad, 1, LANES)

    @pl.loop(0, owner_rows)
    def _(t):
        tz = (t * nz) // owner_rows

        @pl.when(tz != z)
        def _():
            remote(
                send_order.at[t], got_order.at[z], order_send, order_recv, tz, xc
            ).start()

    @pl.when(is_owner)
    def _():
        got_rows[me] = send_rows[my_place]
        got_order[z] = send_order[owner_row]
        drain(got_order.at[pl.ds(0, nz - 1)], order_recv)
        drain(got_rows.at[pl.ds(0, blocks - 1)], rows_recv)
        members = got_rows[...].reshape(blocks, SLOTS * width)
        arrived = got_order[...].reshape(nz, LANES)
        spread = [
            jnp.concatenate(
                [
                    jnp.broadcast_to(
                        arrived[:, n * share + s : n * share + s + 1], (nz, LANES)
                    )
                    for n in range(side)
                ],
                axis=0,
            )
            for s in range(SLOTS)
        ]
        half = iota((blocks, LANES), 1) < LANES // SLOTS
        stamps = jnp.where(half, spread[0], spread[1])
        flipped = jnp.transpose(stamps)
        values = []
        for s in range(SLOTS):
            rows = members[:, s * width : (s + 1) * width]
            at = s * (LANES // SLOTS)
            mine = stamps[:, at : at + 1]
            theirs = flipped[at : at + 1, :]
            gram = lax.dot_general(
                rows, rows, (((1,), (1,)), ((), ())), preferred_element_type=F32
            )
            earlier = (theirs > 0.0) & (theirs < mine)
            values.append(
                jnp.max(jnp.where(earlier, gram, -1.0), axis=1, keepdims=True)
            )
            total = jnp.sum(
                jnp.where(theirs > 0.0, 1.0, 0.0), axis=1, keepdims=True
            )
            summed = jnp.dot(
                jnp.ones((8, blocks), BF16), rows, preferred_element_type=F32
            )[0:1]
            centre = summed / jnp.maximum(total, 1.0)
            offset = rows.astype(F32) - centre
            values.append(jnp.sum(offset * offset, axis=1, keepdims=True))
        kind = lax.rem(iota((blocks, LANES), 1), len(values))
        answer = values[-1]
        for n in range(len(values) - 1):
            answer = jnp.where(kind == n, values[n], answer)
        answers[...] = answer

        @pl.loop(1, side)
        def _(k):
            remote(
                answers.at[pl.ds(pl.multiple_of(beside(k) * nz, nz), nz)],
                gathered.at[xc],
                answer_send,
                answer_recv,
                z,
                beside(k),
            ).start()

        gathered[xc] = answers[pl.ds(pl.multiple_of(xc * nz, nz), nz), :]
        drain(gathered.at[pl.ds(0, side - 1)], answer_recv)
        source = iota((nz, LANES), 1) // share
        packed = gathered[side - 1]
        for n in range(side - 1):
            packed = jnp.where(source == n, gathered[n], packed)
        send_back[...] = packed.reshape(nz, 1, LANES)

        @pl.loop(0, nz)
        def _(tz):
            @pl.when(tz != z)
            def _():
                remote(
                    send_back.at[tz],
                    got_back.at[owner_row],
                    back_send,
                    back_recv,
                    tz,
                    xc,
                ).start()

        got_back[owner_row] = send_back[z]
        drain(got_back.at[pl.ds(0, owner_rows - 1)], back_recv)

    @pl.when(jnp.logical_not(is_owner))
    def _():
        drain(got_back, back_recv)

    back = got_back[...].reshape(owner_rows, LANES)
    columns = jnp.transpose(
        jnp.concatenate(
            [back, jnp.zeros((LANES - owner_rows, LANES), F32)], axis=0
        )
    )
    owner = jnp.floor(slot * (1.0 / SLOTS))
    at_row = jnp.floor(owner * (1.0 / side))
    at_lane = (owner - at_row * side) * share + (slot - owner * SLOTS) * 2.0
    picked = jnp.zeros((LANES, count), F32)
    for t in range(owner_rows):
        picked = jnp.where(at_row == float(t), columns[:, t : t + 1], picked)
    lane = iota((LANES, count), 0).astype(F32)
    best_ref[...] = jnp.sum(
        jnp.where(lane == at_lane, picked, 0.0), axis=0, keepdims=True
    )
    dist_ref[...] = jnp.sum(
        jnp.where(lane == at_lane + 1.0, picked, 0.0), axis=0, keepdims=True
    )

    @pl.when(z < nz - 1)
    def _():
        drain(used_in, used_recv)

        @pl.loop(0, z + 1)
        def _(tz):
            drain(named.at[tz], named_send)

    @pl.when(z == nz - 1)
    def _():
        @pl.loop(0, nz - 1)
        def _(tz):
            drain(used_out, used_send)

    used_ref[...] = used_in[...]
    drain(flags_in.at[pl.ds(0, side - 1)], flag_send)
    drain(order_mid.at[pl.ds(0, side - 1)], mid_send)

    @pl.when(is_owner)
    def _():
        drain(send_rows.at[pl.ds(0, owners - 1)], rows_send)
        drain(send_order.at[pl.ds(0, owner_rows - 1)], order_send)
        drain(gathered.at[pl.ds(0, side - 1)], answer_send)
        drain(send_back.at[pl.ds(0, nz - 1)], back_send)

    @pl.when(jnp.logical_not(is_owner))
    def _():
        drain(send_rows, rows_send)
        drain(send_order.at[pl.ds(0, owner_rows)], order_send)


def one_round(sizes, embeddings, cluster, order, base):
    nz, nx, nc, owner_rows = sizes
    side = nx * nc
    blocks = nz * side
    owners = owner_rows * side
    count, width = embeddings.shape
    tiles = SLOTS * width // LANES
    groups = CLUSTERS // LANES
    vmem = pl.BlockSpec(memory_space=pltpu.VMEM)
    row = jax.ShapeDtypeStruct((1, count), F32)
    dma = pltpu.SemaphoreType.DMA
    inputs = (embeddings, cluster, order)
    if base is None:

        def body(emb_ref, cluster_ref, order_ref, *refs):
            kernel(sizes, emb_ref, cluster_ref, order_ref, None, *refs)

    else:
        inputs += (base,)
        body = functools.partial(kernel, sizes)
    return pl.pallas_call(
        body,
        out_shape=(row, row, jax.ShapeDtypeStruct((1, LANES), F32), row),
        in_specs=[vmem] * len(inputs),
        out_specs=(vmem,) * 4,
        scratch_shapes=[
            pltpu.VMEM((groups, LANES), F32),
            pltpu.VMEM((side, groups, LANES), F32),
            pltpu.VMEM((nz, groups, LANES), F32),
            pltpu.VMEM((1, LANES), F32),
            pltpu.VMEM((1, LANES), F32),
            pltpu.VMEM((owners, tiles, LANES), BF16),
            pltpu.VMEM((side * padded(owner_rows), LANES), F32),
            pltpu.VMEM((side, padded(owner_rows), LANES), F32),
            pltpu.VMEM((padded(owner_rows), 1, LANES), F32),
            pltpu.VMEM((blocks, tiles, LANES), BF16),
            pltpu.VMEM((nz, 1, LANES), F32),
            pltpu.VMEM((blocks, LANES), F32),
            pltpu.VMEM((side, nz, LANES), F32),
            pltpu.VMEM((nz, 1, LANES), F32),
            pltpu.VMEM((owner_rows, 1, LANES), F32),
            pltpu.SemaphoreType.REGULAR((nz,)),
            pltpu.SemaphoreType.REGULAR,
            dma((nz,)),
        ]
        + [dma] * 15,
        compiler_params=pltpu.CompilerParams(
            collective_id=0 if base is None else 1, has_side_effects=True
        ),
    )(*inputs)


def per_device(embeddings, assignment, order):
    nz, nx, nc = (lax.axis_size(a) for a in ("rows", "sub", "pair"))
    count = embeddings.shape[0]
    capacity = count + count // 4
    owner_rows = capacity // (SLOTS * nx * nc)
    capacity = owner_rows * SLOTS * nx * nc
    sizes = (nz, nx, nc, owner_rows)
    run = functools.partial(
        one_round,
        sizes,
        embeddings,
        assignment.reshape(1, count),
        order.reshape(1, count),
    )
    best, dist, used, _ = run(None)

    def unfinished(state):
        return state[2] < used[0, 0]

    def next_round(state):
        best, dist, base = state
        more_best, more_dist, _, rank = run(jnp.full((1, count), base))
        late = (rank >= base) & (rank < base + capacity)
        return (
            jnp.where(late, more_best, best),
            jnp.where(late, more_dist, dist),
            base + capacity,
        )

    best, dist, _ = lax.while_loop(
        unfinished, next_round, (best, dist, jnp.float32(capacity))
    )
    return best.reshape(count), dist.reshape(count)


def solution(mesh):
    in_specs = (
        P(("groups", "rows", "sub", "pair"), None),
        P(("groups", "rows", "sub", "pair")),
        P(("groups", "rows", "sub", "pair")),
    )
    out_specs = (P(("groups", "rows", "sub", "pair")), P(("groups", "rows", "sub", "pair")))
    return jax.shard_map(
        per_device, mesh=mesh, in_specs=in_specs, out_specs=out_specs, check_vma=False
    )
```

time: 150 us -> 117 us (0.78)
  Pallas kernels: 146 us -> 114 us
    pallas_call x1, Pallas kernels: 146 us -> 114 us  [one_round(): pl.pallas_call(body, out_shape=(row, row, jax.ShapeDtypeStruct((1, LANES)...]
where the time goes in v2:
time: 117 us
  Pallas kernels  114 us (97%)
  local copies, waits for them, and re-layouts  2.41 us (2%)
    pallas_call x1, Pallas kernels, one_round(): pl.pallas_call(body, out_shape=(row, row, jax.ShapeDtypeStruct((1, LANES)...  114 us

profile of v2, /device:TPU:65, one launch (start us, length us, event | category | flops | bytes accessed | tf_op | source)
XLA Modules:
  0.0 116.7 jit_solution(6464145681973979123)
XLA Ops:
  0.6 0.0 copy-start
  0.6 113.6 %shard_map.50 = (f32[1,256]{1,0:T(1,128)S(1)}, f32[1,256]{1,0:T(1,128)S(1)}, f32[1,128]{1,0:T(1,128)}, f32[1,256]{1,0:T(1,128)}) custom-call(bf16[256,1024]{1,0:T(8,128)(2,1)} %emb_ref.1, s32[1,256]{1,0:T(1,128)} %bitcast.8, s32[1,256]{1,0:T(1,128)} %bitcast.10), custom_call_target="tpu_custom_call" | custom-call | tf_op jit(solution)/shard_map/pallas_call | solution.py:457
  114.3 0.0 copy-start.2
  114.3 0.0 copy-start.1
  114.3 0.0 copy-done
  114.3 0.6 copy-done.2
  114.9 0.0 copy-done.1
  115.0 0.6 while.12
  115.0 0.0 copy-start.6
  115.0 0.6 copy-done.6
  115.6 0.6 copy.16
  116.2 0.6 copy.17
Async XLA Ops:
  0.6 113.7 %copy-start = (bf16[256,1024]{1,0:T(8,128)(2,1)S(1)}, bf16[256,1024]{1,0:T(8,128)(2,1)}, u32[]{:S(2)}) copy-start(bf16[256,1024]{1,0:T(8,128)(2,1)} %emb_ref.1) | copy-start | bytes 1572868
  114.3 0.7 copy-start.2
  114.3 0.7 copy-start.1
  115.0 0.6 copy-start.6

commit v3 on v2

v3 whole, which is shorter than its diff:
```python
import functools

import jax
import jax.numpy as jnp
from jax import lax
from jax.experimental import pallas as pl
from jax.experimental.pallas import tpu as pltpu
from jax.sharding import PartitionSpec as P

EPSILON = 1e-06
LANES = 128
CLUSTERS = 1024
SLOTS = 2
SPARSE = 4
MESH = pl.DeviceIdType.MESH
F32 = jnp.float32
BF16 = jnp.bfloat16


def iota(shape, dim):
    return lax.broadcasted_iota(jnp.int32, shape, dim)


def drain(ref, sem):
    pltpu.make_async_copy(ref, ref, sem).wait()


def kernel(
    sizes,
    emb_ref,
    cluster_ref,
    order_ref,
    base_ref,
    best_ref,
    dist_ref,
    used_ref,
    rank_ref,
    flags_out,
    flags_in,
    named,
    used_in,
    used_out,
    send_rows,
    send_doubles,
    order_out,
    order_mid,
    send_order,
    got_rows,
    got_doubles,
    got_order,
    answers,
    gathered,
    send_back,
    got_back,
    ready,
    next_in,
    named_recv,
    flag_send,
    flag_recv,
    named_send,
    used_send,
    used_recv,
    rows_send,
    rows_recv,
    doubles_send,
    doubles_recv,
    mid_send,
    mid_recv,
    order_send,
    order_recv,
    answer_send,
    answer_recv,
    back_send,
    back_recv,
):
    nz, nx, nc = sizes
    side = nx * nc
    blocks = nz * side
    doubles = side // SPARSE
    share = LANES // side
    count, width = emb_ref.shape
    pieces = width // LANES
    z = lax.rem(lax.axis_index("rows") + nz - 1, nz)
    x = lax.axis_index("sub")
    c = lax.axis_index("pair")
    xc = x * nc + c
    me = xc * nz + z
    my_place = z * side + xc
    my_double = z * doubles + xc // SPARSE
    is_double = lax.rem(xc, SPARSE) == 0

    def device(tz, txc):
        return {
            "rows": lax.rem(tz + 1, nz),
            "sub": txc // nc,
            "pair": lax.rem(txc, nc),
        }

    def beside(k):
        return lax.rem(xc + k, side)

    def signal(sem, tz, txc):
        pl.semaphore_signal(sem, inc=1, device_id=device(tz, txc), device_id_type=MESH)

    def remote(src, dst, send, recv, tz, txc):
        return pltpu.make_async_remote_copy(
            src_ref=src,
            dst_ref=dst,
            send_sem=send,
            recv_sem=recv,
            device_id=device(tz, txc),
            device_id_type=MESH,
        )

    barrier = pltpu.get_barrier_semaphore()

    @pl.loop(1, side)
    def _(k):
        signal(barrier, z, beside(k))

    @pl.when(z < nz - 1)
    def _():
        signal(barrier, z + 1, xc)

    cluster = cluster_ref[...]
    high = cluster // LANES
    low = cluster - high * LANES
    groups = CLUSTERS // LANES
    is_high = iota((groups, count), 0) == high
    is_low = (iota((LANES, count), 0) == low).astype(F32).astype(BF16)
    flags_out[...] = lax.dot_general(
        is_high.astype(F32).astype(BF16),
        is_low,
        (((1,), (1,)), ((), ())),
        preferred_element_type=F32,
    )

    pl.semaphore_wait(barrier, side - 1 + (z + nz - 1) // nz)

    @pl.when(z > 0)
    def _():
        signal(next_in, z - 1, xc)

    @pl.loop(1, side)
    def _(k):
        remote(flags_out, flags_in.at[xc], flag_send, flag_recv, z, beside(k)).start()

    flags_in[xc] = flags_out[...]

    values = emb_ref[...].astype(F32)
    unit = (
        values * lax.rsqrt(jnp.sum(values * values, axis=1, keepdims=True) + EPSILON)
    ).astype(BF16)

    drain(flags_in.at[pl.ds(0, side - 1)], flag_recv)
    named[z] = jnp.max(flags_in[...], axis=0)

    def pass_on(tz):
        @pl.when(z < nz - 1)
        def _():
            remote(
                named.at[tz], named.at[tz], named_send, named_recv.at[tz], z + 1, xc
            ).start()

    @pl.when(z < nz - 1)
    def _():
        pl.semaphore_wait(next_in, 1)

    @pl.loop(0, z)
    def _(tz):
        drain(named.at[tz], named_recv.at[tz])
        pass_on(tz)
        signal(ready.at[z], tz, xc)

    pass_on(z)

    seen = jnp.zeros((groups, LANES), F32)
    fresh = []
    for tz in range(nz):
        here = jnp.where(z >= tz, named[tz], 0.0)
        fresh.append(jnp.where((here > 0.0) & (seen == 0.0), 1.0, 0.0))
        seen = jnp.maximum(seen, here)
    firsts = jnp.concatenate(fresh, axis=0).astype(BF16)
    levels = nz * groups
    upper = (iota((LANES, LANES), 0) < iota((LANES, LANES), 1)).astype(F32).astype(BF16)
    lower = (iota((levels, levels), 0) > iota((levels, levels), 1)).astype(F32)
    inside = jnp.dot(firsts, upper, preferred_element_type=F32)
    above = jnp.sum(
        jnp.dot(lower.astype(BF16), firsts, preferred_element_type=F32),
        axis=1,
        keepdims=True,
    )
    ranks = inside + above + 1.0
    table = jnp.zeros((groups, LANES), F32)
    for tz in range(nz):
        table += fresh[tz] * ranks[tz * groups : (tz + 1) * groups]

    used = jnp.broadcast_to(jnp.max(table, axis=(0, 1), keepdims=True), used_out.shape)
    used_out[...] = used

    @pl.when(z == nz - 1)
    def _():
        used_in[...] = used

        @pl.loop(0, nz - 1)
        def _(tz):
            remote(used_out, used_in, used_send, used_recv, tz, xc).start()

    tens = jnp.floor(table * (1.0 / 32.0))
    both = jnp.concatenate([tens, table - tens * 32.0], axis=0).astype(BF16)
    found = jnp.dot(both, is_low, preferred_element_type=F32)
    found = found[0:groups] * 32.0 + found[groups:]
    rank = jnp.sum(jnp.where(is_high, found, 0.0), axis=0, keepdims=True) - 1.0
    rank_ref[...] = rank
    slot = rank if base_ref is None else rank - base_ref[...]
    wanted = [
        iota((blocks, count), 0).astype(F32) == slot,
        iota((nz * doubles, count), 0).astype(F32) + float(blocks) == slot,
    ]
    for w, send in zip(wanted, (send_rows, send_doubles)):
        tiles = jnp.dot(w.astype(F32).astype(BF16), unit, preferred_element_type=F32)
        send[...] = tiles.reshape(w.shape[0], pieces, LANES).astype(BF16)
    position = order_ref[...].astype(F32) + 1.0
    line = iota((blocks, count), 0)
    at_row = lax.rem(line, nz)
    column = line // nz
    places = [
        at_row * side + column,
        jnp.where(
            lax.rem(column, SPARSE) == 0,
            blocks + at_row * doubles + column // SPARSE,
            -CLUSTERS,
        ),
    ]
    orders = [
        jnp.sum(jnp.where(p.astype(F32) == slot, position, 0.0), axis=1, keepdims=True)
        for p in places
    ]
    even = lax.rem(iota((blocks, LANES), 1), SLOTS) == 0
    order_out[...] = jnp.where(even, orders[0], orders[1])

    @pl.loop(1, side, unroll=3)
    def _(k):
        remote(
            order_out.at[pl.ds(pl.multiple_of(beside(k) * nz, nz), nz)],
            order_mid.at[xc],
            mid_send,
            mid_recv,
            z,
            beside(k),
        ).start()

    order_mid[xc] = order_out[pl.ds(pl.multiple_of(xc * nz, nz), nz), :]

    def deliver(tz, txc):
        remote(
            send_rows.at[tz * side + txc], got_rows.at[me], rows_send, rows_recv, tz, txc
        ).start()

    def deliver_double(tz, q):
        remote(
            send_doubles.at[tz * doubles + q],
            got_doubles.at[me],
            doubles_send,
            doubles_recv,
            tz,
            q * SPARSE,
        ).start()

    @pl.loop(0, nz)
    def _(tz):
        @pl.when(tz > z)
        def _():
            pl.semaphore_wait(ready.at[tz], 1)

        @pl.loop(1, side, unroll=5)
        def _(k):
            deliver(tz, beside(k))

        @pl.when(tz != z)
        def _():
            deliver(tz, xc)

            @pl.loop(0, doubles)
            def _(q):
                deliver_double(tz, q)

        @pl.when(tz == z)
        def _():
            @pl.loop(0, doubles)
            def _(q):
                @pl.when(q * SPARSE != xc)
                def _():
                    deliver_double(tz, q)

    drain(order_mid.at[pl.ds(0, side - 1)], mid_recv)
    origin = iota((nz, LANES), 1) // share
    packed = order_mid[side - 1]
    for n in range(side - 1):
        packed = jnp.where(origin == n, order_mid[n], packed)
    send_order[...] = packed.reshape(nz, 1, LANES)

    @pl.loop(0, nz)
    def _(tz):
        @pl.when(tz != z)
        def _():
            remote(
                send_order.at[tz], got_order.at[z], order_send, order_recv, tz, xc
            ).start()

    got_rows[me] = send_rows[my_place]
    got_order[z] = send_order[z]
    drain(got_order.at[pl.ds(0, nz - 1)], order_recv)
    arrived = got_order[...].reshape(nz, LANES)
    kind = lax.rem(iota((blocks, LANES), 1), 2 * SLOTS)

    def judge(s, got):
        rows = got[...].reshape(blocks, width)
        stamps = jnp.concatenate(
            [
                jnp.broadcast_to(
                    arrived[:, n * share + s : n * share + s + 1], (nz, LANES)
                )
                for n in range(side)
            ],
            axis=0,
        )
        mine = stamps[:, 0:1]
        theirs = jnp.transpose(stamps)[0:1, :]
        gram = lax.dot_general(
            rows, rows, (((1,), (1,)), ((), ())), preferred_element_type=F32
        )
        earlier = (theirs > 0.0) & (theirs < mine)
        nearest = jnp.max(jnp.where(earlier, gram, -1.0), axis=1, keepdims=True)
        total = jnp.sum(jnp.where(theirs > 0.0, 1.0, 0.0), axis=1, keepdims=True)
        summed = jnp.dot(
            jnp.ones((8, blocks), BF16), rows, preferred_element_type=F32
        )[0:1]
        offset = rows.astype(F32) - summed / jnp.maximum(total, 1.0)
        apart = jnp.sum(offset * offset, axis=1, keepdims=True)
        return nearest, apart

    drain(got_rows.at[pl.ds(0, blocks - 1)], rows_recv)
    nearest, apart = judge(0, got_rows)
    answers[...] = jnp.where(kind == 0, nearest, apart)

    @pl.when(is_double)
    def _():
        got_doubles[me] = send_doubles[my_double]
        drain(got_doubles.at[pl.ds(0, blocks - 1)], doubles_recv)
        nearest, apart = judge(1, got_doubles)
        answers[...] = jnp.where(
            kind == 2, nearest, jnp.where(kind == 3, apart, answers[...])
        )

    @pl.loop(1, side, unroll=3)
    def _(k):
        remote(
            answers.at[pl.ds(pl.multiple_of(beside(k) * nz, nz), nz)],
            gathered.at[xc],
            answer_send,
            answer_recv,
            z,
            beside(k),
        ).start()

    gathered[xc] = answers[pl.ds(pl.multiple_of(xc * nz, nz), nz), :]
    drain(gathered.at[pl.ds(0, side - 1)], answer_recv)
    source = iota((nz, LANES), 1) // share
    packed = gathered[side - 1]
    for n in range(side - 1):
        packed = jnp.where(source == n, gathered[n], packed)
    send_back[...] = packed.reshape(nz, 1, LANES)

    @pl.loop(0, nz)
    def _(tz):
        @pl.when(tz != z)
        def _():
            remote(
                send_back.at[tz], got_back.at[z], back_send, back_recv, tz, xc
            ).start()

    got_back[z] = send_back[z]
    drain(got_back.at[pl.ds(0, nz - 1)], back_recv)

    back = got_back[...].reshape(nz, LANES)
    columns = jnp.transpose(
        jnp.concatenate([back, jnp.zeros((LANES - nz, LANES), F32)], axis=0)
    )
    double = slot >= float(blocks)
    per_row = jnp.where(double, float(doubles), float(side))
    index = jnp.where(double, slot - float(blocks), slot)
    at_row = jnp.floor(index / per_row)
    step = jnp.where(double, float(SPARSE * share), float(share))
    at_lane = (index - at_row * per_row) * step + jnp.where(double, 2.0, 0.0)
    picked = jnp.zeros((LANES, count), F32)
    for t in range(nz):
        picked = jnp.where(at_row == float(t), columns[:, t : t + 1], picked)
    lane = iota((LANES, count), 0).astype(F32)
    best_ref[...] = jnp.sum(
        jnp.where(lane == at_lane, picked, 0.0), axis=0, keepdims=True
    )
    dist_ref[...] = jnp.sum(
        jnp.where(lane == at_lane + 1.0, picked, 0.0), axis=0, keepdims=True
    )

    @pl.when(z < nz - 1)
    def _():
        drain(used_in, used_recv)

        @pl.loop(0, z + 1)
        def _(tz):
            drain(named.at[tz], named_send)

    @pl.when(z == nz - 1)
    def _():
        @pl.loop(0, nz - 1)
        def _(tz):
            drain(used_out, used_send)

    used_ref[...] = used_in[...]
    drain(flags_in.at[pl.ds(0, side - 1)], flag_send)
    drain(order_mid.at[pl.ds(0, side - 1)], mid_send)
    drain(gathered.at[pl.ds(0, side - 1)], answer_send)
    drain(send_order.at[pl.ds(0, nz - 1)], order_send)
    drain(send_back.at[pl.ds(0, nz - 1)], back_send)
    drain(send_rows.at[pl.ds(0, blocks - 1)], rows_send)
    drain(send_doubles.at[pl.ds(0, nz * doubles - 1)], doubles_send)

    @pl.when(jnp.logical_not(is_double))
    def _():
        drain(send_doubles.at[0], doubles_send)


def one_round(sizes, embeddings, cluster, order, base):
    nz, nx, nc = sizes
    side = nx * nc
    blocks = nz * side
    doubles = blocks // SPARSE
    count, width = embeddings.shape
    pieces = width // LANES
    groups = CLUSTERS // LANES
    vmem = pl.BlockSpec(memory_space=pltpu.VMEM)
    row = jax.ShapeDtypeStruct((1, count), F32)
    dma = pltpu.SemaphoreType.DMA
    inputs = (embeddings, cluster, order)
    if base is None:

        def body(emb_ref, cluster_ref, order_ref, *refs):
            kernel(sizes, emb_ref, cluster_ref, order_ref, None, *refs)

    else:
        inputs += (base,)
        body = functools.partial(kernel, sizes)
    return pl.pallas_call(
        body,
        out_shape=(row, row, jax.ShapeDtypeStruct((1, LANES), F32), row),
        in_specs=[vmem] * len(inputs),
        out_specs=(vmem,) * 4,
        scratch_shapes=[
            pltpu.VMEM((groups, LANES), F32),
            pltpu.VMEM((side, groups, LANES), F32),
            pltpu.VMEM((nz, groups, LANES), F32),
            pltpu.VMEM((1, LANES), F32),
            pltpu.VMEM((1, LANES), F32),
            pltpu.VMEM((blocks, pieces, LANES), BF16),
            pltpu.VMEM((doubles, pieces, LANES), BF16),
            pltpu.VMEM((blocks, LANES), F32),
            pltpu.VMEM((side, nz, LANES), F32),
            pltpu.VMEM((nz, 1, LANES), F32),
            pltpu.VMEM((blocks, pieces, LANES), BF16),
            pltpu.VMEM((blocks, pieces, LANES), BF16),
            pltpu.VMEM((nz, 1, LANES), F32),
            pltpu.VMEM((blocks, LANES), F32),
            pltpu.VMEM((side, nz, LANES), F32),
            pltpu.VMEM((nz, 1, LANES), F32),
            pltpu.VMEM((nz, 1, LANES), F32),
            pltpu.SemaphoreType.REGULAR((nz,)),
            pltpu.SemaphoreType.REGULAR,
            dma((nz,)),
        ]
        + [dma] * 17,
        compiler_params=pltpu.CompilerParams(
            collective_id=0 if base is None else 1, has_side_effects=True
        ),
    )(*inputs)


def per_device(embeddings, assignment, order):
    nz, nx, nc = (lax.axis_size(a) for a in ("rows", "sub", "pair"))
    count = embeddings.shape[0]
    capacity = nz * nx * nc + nz * nx * nc // SPARSE
    sizes = (nz, nx, nc)
    run = functools.partial(
        one_round,
        sizes,
        embeddings,
        assignment.reshape(1, count),
        order.reshape(1, count),
    )
    best, dist, used, _ = run(None)

    def unfinished(state):
        return state[2] < used[0, 0]

    def next_round(state):
        best, dist, base = state
        more_best, more_dist, _, rank = run(jnp.full((1, count), base))
        late = (rank >= base) & (rank < base + capacity)
        return (
            jnp.where(late, more_best, best),
            jnp.where(late, more_dist, dist),
            base + capacity,
        )

    best, dist, _ = lax.while_loop(
        unfinished, next_round, (best, dist, jnp.float32(capacity))
    )
    return best.reshape(count), dist.reshape(count)


def solution(mesh):
    in_specs = (
        P(("groups", "rows", "sub", "pair"), None),
        P(("groups", "rows", "sub", "pair")),
        P(("groups", "rows", "sub", "pair")),
    )
    out_specs = (P(("groups", "rows", "sub", "pair")), P(("groups", "rows", "sub", "pair")))
    return jax.shard_map(
        per_device, mesh=mesh, in_specs=in_specs, out_specs=out_specs, check_vma=False
    )
```

time: 117 us -> 111 us (0.949)
  Pallas kernels: 114 us -> 108 us
    pallas_call x1, Pallas kernels: 114 us -> 108 us  [one_round(): pl.pallas_call(body, out_shape=(row, row, jax.ShapeDtypeStruct((1, LANES)...]
where the time goes in v3:
time: 111 us
  Pallas kernels  108 us (97%)
  local copies, waits for them, and re-layouts  2.41 us (2%)
    pallas_call x1, Pallas kernels, one_round(): pl.pallas_call(body, out_shape=(row, row, jax.ShapeDtypeStruct((1, LANES)...  108 us

profile of v3, /device:TPU:65, one launch (start us, length us, event | category | flops | bytes accessed | tf_op | source)
XLA Modules:
  0.0 111.0 jit_solution(12376747966036537164)
XLA Ops:
  0.6 0.0 copy-start
  0.6 107.9 %shard_map.50 = (f32[1,256]{1,0:T(1,128)S(1)}, f32[1,256]{1,0:T(1,128)S(1)}, f32[1,128]{1,0:T(1,128)}, f32[1,256]{1,0:T(1,128)}) custom-call(bf16[256,1024]{1,0:T(8,128)(2,1)} %emb_ref.1, s32[1,256]{1,0:T(1,128)} %bitcast.8, s32[1,256]{1,0:T(1,128)} %bitcast.10), custom_call_target="tpu_custom_call" | custom-call | tf_op jit(solution)/shard_map/pallas_call | solution.py:455
  108.5 0.0 copy-start.2
  108.5 0.0 copy-start.1
  108.5 0.0 copy-done
  108.5 0.6 copy-done.2
  109.2 0.0 copy-done.1
  109.2 0.6 while.12
  109.2 0.0 copy-start.6
  109.2 0.6 copy-done.6
  109.9 0.6 copy.16
  110.4 0.6 copy.17
Async XLA Ops:
  0.6 107.9 %copy-start = (bf16[256,1024]{1,0:T(8,128)(2,1)S(1)}, bf16[256,1024]{1,0:T(8,128)(2,1)}, u32[]{:S(2)}) copy-start(bf16[256,1024]{1,0:T(8,128)(2,1)} %emb_ref.1) | copy-start | bytes 1572868
  108.5 0.7 copy-start.2
  108.5 0.7 copy-start.1
  109.2 0.6 copy-start.6

commit v4 on v3

--- a/solution.py
+++ b/solution.py
@@ -267,8 +267,13 @@
             q * SPARSE,
         ).start()
 
+    late = z // (nz - nz // 4)
+
     @pl.loop(0, nz)
-    def _(tz):
+    def _(turn):
+        away = nz // 2 + ((turn + 1) // 2) * (1 - 2 * lax.rem(turn, 2))
+        tz = turn + (lax.rem(z + away, nz) - turn) * late
+
         @pl.when(tz > z)
         def _():
             pl.semaphore_wait(ready.at[tz], 1)

time: 111 us -> 108 us (0.973)
  Pallas kernels: 108 us -> 105 us
    pallas_call x1, Pallas kernels: 108 us -> 105 us  [one_round(): pl.pallas_call(body, out_shape=(row, row, jax.ShapeDtypeStruct((1, LANES)...]
where the time goes in v4:
time: 108 us
  Pallas kernels  105 us (97%)
  local copies, waits for them, and re-layouts  2.41 us (2%)
    pallas_call x1, Pallas kernels, one_round(): pl.pallas_call(body, out_shape=(row, row, jax.ShapeDtypeStruct((1, LANES)...  105 us

profile of v4, /device:TPU:65, one launch (start us, length us, event | category | flops | bytes accessed | tf_op | source)
XLA Modules:
  0.0 108.2 jit_solution(11260814054286511949)
XLA Ops:
  0.6 0.0 copy-start
  0.6 105.0 %shard_map.50 = (f32[1,256]{1,0:T(1,128)S(1)}, f32[1,256]{1,0:T(1,128)S(1)}, f32[1,128]{1,0:T(1,128)}, f32[1,256]{1,0:T(1,128)}) custom-call(bf16[256,1024]{1,0:T(8,128)(2,1)} %emb_ref.1, s32[1,256]{1,0:T(1,128)} %bitcast.8, s32[1,256]{1,0:T(1,128)} %bitcast.10), custom_call_target="tpu_custom_call" | custom-call | tf_op jit(solution)/shard_map/pallas_call | solution.py:460
  105.7 0.0 copy-start.2
  105.7 0.0 copy-start.1
  105.7 0.0 copy-done
  105.7 0.6 copy-done.2
  106.4 0.0 copy-done.1
  106.4 0.6 while.12
  106.4 0.0 copy-start.6
  106.4 0.6 copy-done.6
  107.0 0.6 copy.16
  107.6 0.6 copy.17
Async XLA Ops:
  0.6 105.1 %copy-start = (bf16[256,1024]{1,0:T(8,128)(2,1)S(1)}, bf16[256,1024]{1,0:T(8,128)(2,1)}, u32[]{:S(2)}) copy-start(bf16[256,1024]{1,0:T(8,128)(2,1)} %emb_ref.1) | copy-start | bytes 1572868
  105.7 0.7 copy-start.2
  105.7 0.7 copy-start.1
  106.4 0.6 copy-start.6
